TPU v7x, 512 devices: a whole 4x8x8 slice. The times are simulated.
512 devices in a mesh: front: 8 (over y), row: 8 (over z), col: 8 (over x, core).
Axes of the slice: x: 4, y: 8, z: 8, core: 2. Of those that a mesh axis runs over, the one named last changes fastest.
Arguments:
- pivot: float32 [8, 512, 512], P('front', ('row', 'col')), may hold values from -1 to 8
- col_ut: bfloat16 [8, 8, 96, 512], P('front', 'row', None, 'col'), may hold values from -6 to 6
- col_vt: bfloat16 [8, 8, 96, 512], P('front', 'row', None, 'col'), may hold values from -0.25 to 0.25
- col_rank: int32 [8, 8], P('front', 'row'), may hold values from 32 to 96
- row_ut: bfloat16 [8, 8, 96, 512], P('front', 'col', None, 'row'), may hold values from -6 to 6
- row_vt: bfloat16 [8, 8, 96, 512], P('front', 'col', None, 'row'), may hold values from -0.625 to 0.625
- row_rank: int32 [8, 8], P('front', 'col'), may hold values from 32 to 96
- cb_ut: bfloat16 [8, 8, 8, 96, 512], P('front', 'row', 'col'), may hold values from -6 to 6
- cb_vt: bfloat16 [8, 8, 8, 96, 512], P('front', 'row', 'col'), may hold values from -0.625 to 0.625
- cb_rank: int32 [8, 8, 8], P('front', 'row', 'col'), may hold values from 32 to 96
- parent_map: int32 [8, 8], P('front'), may hold values from 0 to 15, as said below
Outputs:
- parent_tiles: bfloat16 [8, 16, 8, 512, 512], P('front', 'row', 'col')
Inputs may be any that keep to these rules, and one draw needn't show every extreme that they name: `parent_map`: for every front the entries are distinct; entry 0 is 8, and 0 and 15 both appear.
All inputs are finite; a program needn't handle non-finite values.
Results may differ from a plain program's by a relative error of at most 0.0062.
Values may be sent and summed in bfloat16 or wider, within the bound.
No kernel may reach another device: no remote copies, remote signals or barrier semaphores. Data moves between devices by JAX's collectives and lax.ppermute only.
A program may use at most 64 MiB of HBM per device.

v0:
```python
import jax
import jax.numpy as jnp
from jax import lax
from jax.sharding import PartitionSpec as P

NS_ITERS = 2
HIGH = lax.Precision.HIGHEST


def in_order(blocks, dim):
    blocks = jnp.moveaxis(blocks, 0, dim)
    shape = blocks.shape
    return blocks.reshape(*shape[:dim], shape[dim] * shape[dim + 1], *shape[dim + 2 :])


def copy_for_each(x, axis):
    copies = jnp.broadcast_to(x, (lax.axis_size(axis), *x.shape))
    return lax.all_to_all(copies, axis, split_axis=0, concat_axis=0, tiled=True)


def gather_directly(x, axis, dim):
    return in_order(copy_for_each(x, axis), dim)


def gather_turned(arrays, axis, dims):
    turned = [jnp.moveaxis(a, dim, 0) for a, dim in zip(arrays, dims)]
    widths = [t[0].size for t in turned]
    both = jnp.concatenate([t.reshape(-1, w) for t, w in zip(turned, widths)], axis=1)
    result = lax.all_gather(both, axis, axis=0, tiled=True)
    blocks = jnp.split(result, [sum(widths[:k]) for k in range(1, len(widths))], axis=1)
    return tuple(
        (
            jnp.moveaxis(b.reshape(-1, *t.shape[1:]), 0, dim)
            for b, t, dim in zip(blocks, turned, dims)
        )
    )


def sent_together(arrays, axis, dim, along):
    widths = [a.shape[along] for a in arrays]
    both = jnp.concatenate(arrays, axis=along)
    result = lax.all_gather(both, axis, axis=dim, tiled=True)
    return tuple(jnp.split(result, [sum(widths[:k]) for k in range(1, len(widths))], axis=along))


def swapped(x, axis, bit):
    return lax.ppermute(x, axis, [(i, i ^ 1 << bit) for i in range(lax.axis_size(axis))])


def ranked(factor, rank):
    levels = jnp.arange(factor.shape[-2], dtype=jnp.int32)[:, None]
    keep = levels < rank[..., None, None]
    return jnp.where(keep, factor, jnp.zeros_like(factor))


def densify(left, right):
    return jnp.einsum("ijkx,ijky->ijxy", left, right, preferred_element_type=jnp.float32).astype(
        jnp.bfloat16
    )


def selector(mapping, first, count):
    wanted = first + jnp.arange(count, dtype=jnp.int32)
    return (mapping[None, :] == wanted[:, None]).astype(jnp.bfloat16)


def fold_rows(select_rows, carry, pieces):
    results = []
    for total, piece in zip(carry, pieces):
        count = piece.shape[0]
        flat = piece.reshape(count, -1)
        moved = jnp.dot(select_rows, flat, preferred_element_type=jnp.float32).astype(jnp.bfloat16)
        results.append(moved.reshape(total.shape))
    return tuple(results)


def fold_cols(select_cols, carry, pieces):
    results = []
    for total, piece in zip(carry, pieces):
        count = piece.shape[1]
        flat = piece.reshape(piece.shape[0], count, -1)
        moved = jnp.einsum(
            "bj,ajx->abx", select_cols, flat, preferred_element_type=jnp.float32
        ).astype(jnp.bfloat16)
        results.append(moved.reshape(total.shape))
    return tuple(results)


def shards(
    pivot, col_ut, col_vt, col_rank, row_ut, row_vt, row_rank, cb_ut, cb_vt, cb_rank, parent_map
):
    whole = gather_directly(pivot[0], ("row", "col"), 0)
    eye = jnp.eye(whole.shape[0], dtype=jnp.float32)
    approx = eye / jnp.diagonal(whole)[None, :]
    for step in range(NS_ITERS):
        approx = jnp.dot(approx, 2.0 * eye - jnp.dot(whole, approx, precision=HIGH), precision=HIGH)
    column_left, column_right = gather_turned((col_ut[0], col_vt[0]), "col", (2, 2))
    column_left = ranked(column_left, col_rank[0])
    column_right = ranked(column_right, col_rank[0])
    lower = jnp.einsum(
        "atx,xy->aty", column_right.astype(jnp.float32), approx, precision=HIGH
    ).astype(jnp.bfloat16)
    upper_left, upper_right = gather_turned((row_ut[0], row_vt[0]), "row", (2, 2))
    upper_left = ranked(upper_left, row_rank[0])
    upper_right = ranked(upper_right, row_rank[0])
    core = jnp.einsum(
        "iax,jbx->ijab", lower, upper_left, preferred_element_type=jnp.float32
    ).astype(jnp.bfloat16)
    update = jnp.einsum(
        "ijab,iax->ijbx", core, column_left, preferred_element_type=jnp.float32
    ).astype(jnp.bfloat16)
    block_left = ranked(cb_ut[0], cb_rank[0])
    block_right = ranked(cb_vt[0], cb_rank[0])
    rows_here = block_left.shape[0]
    cols_here = block_left.shape[1]
    left = jnp.concatenate([block_left, -update], axis=2)
    right = jnp.concatenate([block_right, upper_right[None]], axis=2)
    parent_rows = 2 * rows_here
    select_rows = selector(parent_map[0], lax.axis_index("row") * parent_rows, parent_rows)
    select_cols = selector(parent_map[0], lax.axis_index("col") * parent_rows, parent_rows)
    factor_shape = left.shape[2:]
    empty_rows = jnp.zeros((parent_rows, cols_here) + factor_shape, jnp.bfloat16)
    rows_left, rows_right = fold_rows(
        select_rows, (empty_rows, empty_rows), sent_together((left, right), "row", 0, 1)
    )
    empty_cols = jnp.zeros((parent_rows, parent_rows) + factor_shape, jnp.bfloat16)
    both_left, both_right = fold_cols(
        select_cols, (empty_cols, empty_cols), sent_together((rows_left, rows_right), "col", 1, 0)
    )
    placed = densify(both_left, both_right)
    side = lax.axis_index("front") % 2
    mine = lax.dynamic_slice_in_dim(placed, side * cols_here, cols_here, 1)
    other = lax.dynamic_slice_in_dim(placed, (1 - side) * cols_here, cols_here, 1)
    received = swapped(other, "front", 0)
    total = mine.astype(jnp.float32) + received.astype(jnp.float32)
    return total.astype(jnp.bfloat16)[None]


def solution(mesh):
    placed = (
        P("front", ("row", "col"), None),
        P("front", "row", None, "col"),
        P("front", "row", None, "col"),
        P("front", "row"),
        P("front", "col", None, "row"),
        P("front", "col", None, "row"),
        P("front", "col"),
        P("front", "row", "col", None, None),
        P("front", "row", "col", None, None),
        P("front", "row", "col"),
        P("front", None),
    )
    return jax.shard_map(
        shards,
        mesh=mesh,
        in_specs=placed,
        out_specs=P("front", "row", "col", None, None),
        check_vma=False,
    )
```

profile of v0, /device:TPU:1, one launch (start us, length us, event | category | flops | bytes accessed | tf_op | source)
XLA Modules:
  0.0 238.1 jit_solution(16976337831034606800)
XLA Ops:
  6.5 1.8 broadcast_in_dim.49
  8.4 15.0 %all-to-all-start = ((f32[64,8,512]{2,1,0:T(8,128)}), f32[64,8,512]{2,1,0:T(8,128)S(1)}, u32[]{:S(2)}, u32[]{:S(2)}) async-start(f32[64,8,512]{2,1,0:T(8,128)} %broadcast_in_dim.49), calls=%async_computation | async-start | bytes 2097152 | tf_op jit(solution)/shard_map/all_to_all | solution.py:18
  23.4 0.0 all-gather.3.cloned.1.call-start
  23.4 0.1 pad_maximum_fusion.2
  23.5 13.7 %all_gather.13 = bf16[512,192]{1,0:T(8,128)(2,1)S(1)} all-gather(bf16[64,192]{1,0:T(8,128)(2,1)S(1)} %pad_maximum_fusion.2), channel_id=1, replica_groups=mesh['front'=8,'row'=8,'col'=8] {'col'}, dimensions={0}, use_global_device_ids=true | all-gather | bytes 221184 | tf_op jit(solution)/shard_map/all_gather | solution.py:29
  37.2 0.1 fusion.42
  37.3 0.1 copy.34
  38.1 0.1 pad_maximum_fusion.1
  38.2 24.5 %all_gather.12 = bf16[512,192]{1,0:T(8,128)(2,1)S(1)} all-gather(bf16[64,192]{1,0:T(8,128)(2,1)S(1)} %pad_maximum_fusion.1), channel_id=1, replica_groups=mesh['front'=8,'row'=8,'col'=8] {'row'}, dimensions={0}, use_global_device_ids=true | all-gather | bytes 221184 | tf_op jit(solution)/shard_map/all_gather | solution.py:29
  62.7 0.1 fusion.41
  62.8 0.1 copy.33
  62.9 0.1 copy.35
  63.7 0.1 copy.36
  64.5 0.1 fusion.13
  64.6 0.1 bitcast_select_fusion.9
  64.7 4.7 %gather_fusion = f32[512]{0:T(512)S(1)} fusion(f32[512,512]{1,0:T(8,128)S(1)} %bitcast.142, s32[512]{0:T(512)S(1)} %bitcast.141), kind=kCustom, calls=%fused_computation | custom fusion | bytes 8192 | tf_op jit(solution)/shard_map/jit(diagonal)/cond/branch_0_fun/gather | solution.py:94
  69.4 1.9 select_subtract_fusion.1
  71.3 3.6 %fusion.6 = f32[512,512]{1,0:T(8,128)S(1)} fusion(f32[512,512]{0,1:T(8,128)S(1)} %select_subtract_fusion.1, f32[512]{0:T(512)S(1)} %gather_fusion), kind=kOutput, calls=%fused_computation.24 | convolution fusion | flops 1611399168 | bytes 2099200 | tf_op jit(solution)/shard_map/dot_general | solution.py:96
  74.9 3.5 %select_subtract_fusion = f32[512,512]{0,1:T(8,128)S(1)} fusion(f32[512,512]{1,0:T(8,128)S(1)} %fusion.6, f32[64,8,512]{2,1,0:T(8,128)S(1)} %all-to-all-done), kind=kOutput, calls=%fused_computation.11 | convolution fusion | flops 1611399168 | bytes 3145728 | tf_op jit(solution)/shard_map/dot_general | solution.py:96
  78.3 1.9 fusion.43
  80.2 0.5 convolution_convert_fusion.5
  80.8 0.4 fusion.3
  81.1 0.8 maximum_maximum_fusion
  81.9 0.0 all-gather.3.cloned.1.call-update
  81.9 0.3 all-gather.5.cloned.1.call-start
  82.2 53.2 %all-gather.3.cloned.1.call-done = bf16[8,2,192,512]{3,2,1,0:T(8,128)(2,1)} async-done(((bf16[1,2,192,512]{3,2,1,0:T(8,128)(2,1)}), bf16[8,2,192,512]{3,2,1,0:T(8,128)(2,1)}) %all-gather.3.cloned.1.call-update) | async-done | bytes 3145744 | tf_op jit(solution)/shard_map/all_gather | solution.py:42
  135.4 2.1 slice_bitcast_fusion.1
  137.5 0.9 copy.37
  138.4 0.0 copy-start.7
  138.4 0.9 copy.39
  139.3 0.6 convolution_convert_fusion.3
  139.9 0.6 convolution_convert_fusion.2
  140.5 0.1 copy_bitcast_fusion
  140.6 0.9 pad_maximum_fusion
  141.6 0.0 all-gather.5.cloned.1.call-update
  141.6 44.9 %all-gather.5.cloned.1.call-done = bf16[4,8,192,512]{3,2,0,1:T(8,128)(2,1)} async-done(((bf16[4,1,192,512]{3,2,0,1:T(8,128)(2,1)}), bf16[4,8,192,512]{3,2,0,1:T(8,128)(2,1)}) %all-gather.5.cloned.1.call-update) | async-done | bytes 6291472 | tf_op jit(solution)/shard_map/all_gather | solution.py:42
  186.6 3.4 %fusion.40 = (bf16[2,8,192,512]{3,2,0,1:T(8,128)(2,1)S(1)}, bf16[2,8,192,512]{3,2,0,1:T(8,128)(2,1)S(1)}) fusion(bf16[4,8,192,512]{3,2,0,1:T(8,128)(2,1)} %all-gather.5.cloned.1.call-done), kind=kLoop, calls=%fused_computation.73 | loop fusion | bytes 12582912 | tf_op jit(solution)/shard_map/split | solution.py:43
  189.9 1.8 copy.31
  191.7 1.9 fusion.1
  193.6 2.4 %reshape.193 = bf16[2,2,192,512]{3,2,1,0:T(8,128)(2,1)} reshape(bf16[2,2,98304]{2,1,0:T(2,128)(2,1)} %fusion.1) | data formatting | bytes 1572864 | tf_op jit(solution)/shard_map/reshape | solution.py:85
  196.0 1.8 copy.30
  197.8 1.0 fusion
  198.8 1.4 reshape.191
  200.3 1.9 convolution_convert_fusion.4
  202.2 0.1 constant_dynamic-slice_fusion
  202.3 3.1 %collective-permute-start = (bf16[2,1,512,512]{3,2,1,0:T(8,128)(2,1)S(1)}, bf16[2,1,512,512]{3,2,1,0:T(8,128)(2,1)}, u32[]{:S(2)}, u32[]{:S(2)}) collective-permute-start(bf16[2,1,512,512]{3,2,1,0:T(8,128)(2,1)S(1)} %constant_dynamic-slice_fusion), channel_id=1, source_target_pairs={{0,64},{64,0},{128,192},{192,128},{256,320},{320,256},{384,448},{4... | collective-permute-start | bytes 3145736 | tf_op jit(solution)/shard_map/ppermute | solution.py:47
  205.5 23.3 %collective-permute-done = bf16[2,1,512,512]{3,2,1,0:T(8,128)(2,1)} collective-permute-done((bf16[2,1,512,512]{3,2,1,0:T(8,128)(2,1)S(1)}, bf16[2,1,512,512]{3,2,1,0:T(8,128)(2,1)}, u32[]{:S(2)}, u32[]{:S(2)}) %collective-permute-start) | collective-permute-done | bytes 1048608 | tf_op jit(solution)/shard_map/ppermute | solution.py:47
  228.8 2.5 %fusion.5 = bf16[1,2,1,512,512]{4,3,2,1,0:T(8,128)(2,1)} fusion(bf16[2,1,512,512]{3,2,1,0:T(8,128)(2,1)} %collective-permute-done, bf16[2,2,512,512]{3,2,1,0:T(8,128)(2,1)S(1)} %convolution_convert_fusion.4, s32[]{:T(128)S(6)} %select_n.76), kind=kLoop, calls=%fused_computation.21 | loop fusion | flops 2097152 | bytes 3145732 | tf_op jit(solution)/shard_map/broadcast_in_dim | solution.py:136
  (22 shorter events, 0.1 us)
Async XLA Ops:
  6.5 16.9 %copy-start.4 = (bf16[1,1,96,64]{2,3,1,0:T(8,128)(2,1)S(1)}, bf16[1,1,96,64]{2,3,1,0:T(8,128)(2,1)}, u32[]{:S(2)}) copy-start(bf16[1,1,96,64]{2,3,1,0:T(8,128)(2,1)} %param.12) | copy-start | bytes 36868
  6.5 16.9 %copy-start.3 = (bf16[1,1,96,64]{2,3,1,0:T(8,128)(2,1)S(1)}, bf16[1,1,96,64]{2,3,1,0:T(8,128)(2,1)}, u32[]{:S(2)}) copy-start(bf16[1,1,96,64]{2,3,1,0:T(8,128)(2,1)} %param.13) | copy-start | bytes 36868
  6.5 31.6 %copy-start.5 = (bf16[1,1,96,64]{2,3,1,0:T(8,128)(2,1)S(1)}, bf16[1,1,96,64]{2,3,1,0:T(8,128)(2,1)}, u32[]{:S(2)}) copy-start(bf16[1,1,96,64]{2,3,1,0:T(8,128)(2,1)} %param.16) | copy-start | bytes 36868
  6.5 31.6 %copy-start.6 = (bf16[1,1,96,64]{2,3,1,0:T(8,128)(2,1)S(1)}, bf16[1,1,96,64]{2,3,1,0:T(8,128)(2,1)}, u32[]{:S(2)}) copy-start(bf16[1,1,96,64]{2,3,1,0:T(8,128)(2,1)} %param.15) | copy-start | bytes 36868
  8.4 56.2 %copy-start.1 = (bf16[1,1,1,96,512]{4,3,2,1,0:T(8,128)(2,1)S(1)}, bf16[1,1,1,96,512]{4,3,2,1,0:T(8,128)(2,1)}, u32[]{:S(2)}) copy-start(bf16[1,1,1,96,512]{4,3,2,1,0:T(8,128)(2,1)} %param.18) | copy-start | bytes 294916
  8.4 56.2 %copy-start.2 = (bf16[1,1,1,96,512]{4,3,2,1,0:T(8,128)(2,1)S(1)}, bf16[1,1,1,96,512]{4,3,2,1,0:T(8,128)(2,1)}, u32[]{:S(2)}) copy-start(bf16[1,1,1,96,512]{4,3,2,1,0:T(8,128)(2,1)} %param.19) | copy-start | bytes 294916
  8.4 56.3 %all-to-all-start = ((f32[64,8,512]{2,1,0:T(8,128)}), f32[64,8,512]{2,1,0:T(8,128)S(1)}, u32[]{:S(2)}, u32[]{:S(2)}) async-start(f32[64,8,512]{2,1,0:T(8,128)} %broadcast_in_dim.49), calls=%async_computation | async-start | bytes 2097152 | tf_op jit(solution)/shard_map/all_to_all | solution.py:18
  23.4 112.1 %all-gather.3.cloned.1.call-start = ((), (), s32[]{:S(2)}) async-start(), calls=%async_computation.1 | async-start | bytes 3538944 | tf_op jit(solution)/shard_map/all_gather | solution.py:42
  81.9 104.6 %all-gather.5.cloned.1.call-start = ((), (), s32[]{:S(2)}) async-start(), calls=%async_computation.2 | async-start | bytes 7077888 | tf_op jit(solution)/shard_map/all_gather | solution.py:42
  138.4 0.9 copy-start.7
  197.8 2.5 %copy-start = (bf16[2,2,192,512]{3,2,1,0:T(8,128)(2,1)S(1)}, bf16[2,2,192,512]{3,2,1,0:T(8,128)(2,1)}, u32[]{:S(2)}) copy-start(bf16[2,2,192,512]{3,2,1,0:T(8,128)(2,1)} %reshape.193) | copy-start | bytes 2359300
  202.3 26.5 %collective-permute-start = (bf16[2,1,512,512]{3,2,1,0:T(8,128)(2,1)S(1)}, bf16[2,1,512,512]{3,2,1,0:T(8,128)(2,1)}, u32[]{:S(2)}, u32[]{:S(2)}) collective-permute-start(bf16[2,1,512,512]{3,2,1,0:T(8,128)(2,1)S(1)} %constant_dynamic-slice_fusion), channel_id=1, source_target_pairs={{0,64},{64,0},{128,192},{192,128},{256,320},{320,256},{384,448},{4... | collective-permute-start | bytes 3145736 | tf_op jit(solution)/shard_map/ppermute | solution.py:47
Sparse Core Ops, SparseCore 0:
  82.1 53.3 all-gather.2
  141.7 44.8 all-gather.4
where the time goes:
time: 239 us; the launch traced here: 238 us
  waiting for transfers between devices  121 us (51%)
  blocking collectives  38.2 us (16%)
  local copies, waits for them, and re-layouts  21.9 us (9%)
  starting transfers between devices  18.4 us (8%)
  matrix products  17.8 us (7%)
  between operations  15.7 us (7%)
  other arithmetic  4.56 us (2%)
    all_gather x2, waiting for transfers between devices, sent_together(): result = lax.all_gather(both, axis, axis=dim, tiled=True)  98.1 us
    all_gather x2, blocking collectives, gather_turned(): result = lax.all_gather(both, axis, axis=0, tiled=True)  38.2 us
    ppermute x1, waiting for transfers between devices, swapped(): lax.ppermute(x, axis, [(i, i ^ 1 << bit) for i in range(lax.axis_size(axi...  23.3 us
    all_to_all x1, starting transfers between devices, copy_for_each(): return lax.all_to_all(copies, axis, split_axis=0, concat_axis=0, tiled=True)  15 us
    split x3, local copies, waits for them, and re-layouts, sent_together(): jnp.split(result, [sum(widths[:k]) for k in range(1, len(widths))], axis=...  6.87 us
    dot_general x2, matrix products, shards(): jnp.dot(approx, 2.0 * eye - jnp.dot(whole, approx, precision=HIGH), preci...  5.44 us
    dot_general x2, matrix products, shards(): jnp.dot(whole, approx, precision=HIGH)  5.34 us
  transfers between devices with their start and end apart: 4, of which 3 were waited for; matrix products, arithmetic and copies ran while one was open for 0% of the time, Pallas kernels for 0%

commit v1 on v0

--- a/solution.py
+++ b/solution.py
@@ -26,7 +26,9 @@
     turned = [jnp.moveaxis(a, dim, 0) for a, dim in zip(arrays, dims)]
     widths = [t[0].size for t in turned]
     both = jnp.concatenate([t.reshape(-1, w) for t, w in zip(turned, widths)], axis=1)
-    result = lax.all_gather(both, axis, axis=0, tiled=True)
+    result = jnp.concatenate(
+        lax.all_to_all(jnp.stack([both] * lax.axis_size(axis)), axis, 0, 0), axis=0
+    )
     blocks = jnp.split(result, [sum(widths[:k]) for k in range(1, len(widths))], axis=1)
     return tuple(
         (

time: 239 us -> 243 us (1.017)
  waiting for transfers between devices: 121 us -> 144 us
  blocking collectives: 38.2 us -> 15.6 us
    all_gather x2 -> x0, blocking collectives: 38.2 us -> none  [gather_turned(): result = lax.all_gather(both, axis, axis=0, tiled=True)]
    all_to_all x1, waiting for transfers between devices: 0.01 us -> 25.4 us  [copy_for_each(): return lax.all_to_all(copies, axis, split_axis=0, concat_axis=0, tiled=True)]
    all_to_all x0 -> x1, blocking collectives: none -> 15.6 us  [gather_turned(): lax.all_to_all(jnp.stack([both] * lax.axis_size(axis)), axis, 0, 0)]
    all_to_all x0 -> x1, starting transfers between devices: none -> 10.2 us  [gather_turned(): lax.all_to_all(jnp.stack([both] * lax.axis_size(axis)), axis, 0, 0)]
    all_to_all x1, starting transfers between devices: 15 us -> 6.74 us  [copy_for_each(): return lax.all_to_all(copies, axis, split_axis=0, concat_axis=0, tiled=True)]
    all_gather x2, waiting for transfers between devices: 98.1 us -> 90 us  [sent_together(): result = lax.all_gather(both, axis, axis=dim, tiled=True)]
    all_to_all x0 -> x1, waiting for transfers between devices: none -> 5.64 us  [gather_turned(): lax.all_to_all(jnp.stack([both] * lax.axis_size(axis)), axis, 0, 0)]
  transfers between devices with their start and end apart: 4 -> 5, of which waited for: 3 -> 5; matrix products, arithmetic and copies ran while one was open for 0% -> 1% of each run, Pallas kernels for 0% -> 0%
where the time goes in v1:
time: 243 us; the launch traced here: 242 us
  waiting for transfers between devices  144 us (59%)
  local copies, waits for them, and re-layouts  22.4 us (9%)
  starting transfers between devices  20.3 us (8%)
  matrix products  17.9 us (7%)
  between operations  15.7 us (6%)
  blocking collectives  15.6 us (6%)
  other arithmetic  6.07 us (2%)
    all_gather x2, waiting for transfers between devices, sent_together(): result = lax.all_gather(both, axis, axis=dim, tiled=True)  90 us
    all_to_all x1, waiting for transfers between devices, copy_for_each(): return lax.all_to_all(copies, axis, split_axis=0, concat_axis=0, tiled=True)  25.4 us
    ppermute x1, waiting for transfers between devices, swapped(): lax.ppermute(x, axis, [(i, i ^ 1 << bit) for i in range(lax.axis_size(axi...  23.3 us
    all_to_all x1, blocking collectives, gather_turned(): lax.all_to_all(jnp.stack([both] * lax.axis_size(axis)), axis, 0, 0)  15.6 us
    all_to_all x1, starting transfers between devices, gather_turned(): lax.all_to_all(jnp.stack([both] * lax.axis_size(axis)), axis, 0, 0)  10.2 us
    split x3, local copies, waits for them, and re-layouts, sent_together(): jnp.split(result, [sum(widths[:k]) for k in range(1, len(widths))], axis=...  6.87 us
    all_to_all x1, starting transfers between devices, copy_for_each(): return lax.all_to_all(copies, axis, split_axis=0, concat_axis=0, tiled=True)  6.74 us
    all_to_all x1, waiting for transfers between devices, gather_turned(): lax.all_to_all(jnp.stack([both] * lax.axis_size(axis)), axis, 0, 0)  5.64 us
  transfers between devices with their start and end apart: 5, of which 5 were waited for; matrix products, arithmetic and copies ran while one was open for 1% of the time, Pallas kernels for 0%

profile of v1, /device:TPU:1, one launch (start us, length us, event | category | flops | bytes accessed | tf_op | source)
XLA Modules:
  0.0 242.3 jit_solution(15548479821128526202)
XLA Ops:
  6.5 0.8 pad_maximum_fusion.2
  7.3 0.7 stack.5
  8.1 10.2 %all-to-all-start.1 = ((bf16[8,64,192]{2,1,0:T(8,128)(2,1)}), bf16[8,64,192]{2,1,0:T(8,128)(2,1)S(1)}, u32[]{:S(2)}, u32[]{:S(2)}) async-start(bf16[8,64,192]{2,1,0:T(8,128)(2,1)} %stack.5), calls=%async_computation.1 | async-start | bytes 524288 | tf_op jit(solution)/shard_map/all_to_all | solution.py:30
  18.2 0.9 pad_maximum_fusion.1
  19.1 5.6 %all-to-all-done.1 = bf16[8,64,192]{2,1,0:T(8,128)(2,1)S(1)} async-done(((bf16[8,64,192]{2,1,0:T(8,128)(2,1)}), bf16[8,64,192]{2,1,0:T(8,128)(2,1)S(1)}, u32[]{:S(2)}, u32[]{:S(2)}) %all-to-all-start.1) | async-done | bytes 196640 | tf_op jit(solution)/shard_map/all_to_all | solution.py:30
  24.7 15.6 %all_to_all.15 = bf16[8,64,192]{2,1,0:T(8,128)(2,1)S(1)} all-to-all(bf16[8,64,192]{2,1,0:T(8,128)(2,1)S(1)} %stack.4), channel_id=1, replica_groups=mesh['front'=8,'row'=8,'col'=8] {'row'}, dimensions={0} | all-to-all | bytes 393216 | tf_op jit(solution)/shard_map/all_to_all | solution.py:30
  40.4 1.8 broadcast_in_dim.49
  42.2 6.7 %all-to-all-start.2 = ((f32[64,8,512]{2,1,0:T(8,128)}), f32[64,8,512]{2,1,0:T(8,128)S(1)}, u32[]{:S(2)}, u32[]{:S(2)}) async-start(f32[64,8,512]{2,1,0:T(8,128)} %broadcast_in_dim.49), calls=%async_computation.2 | async-start | bytes 2097152 | tf_op jit(solution)/shard_map/all_to_all | solution.py:18
  48.9 0.0 all-gather.3.cloned.1.call-start
  51.0 0.1 bitcast_select_fusion.9
  51.1 0.1 fusion.42
  51.2 0.1 copy.32
  51.3 0.1 copy.33
  51.4 0.1 fusion.41
  51.5 0.1 copy.31
  51.6 0.1 copy.34
  51.8 0.1 fusion.13
  51.8 25.4 %all-to-all-done.2 = f32[64,8,512]{2,1,0:T(8,128)S(1)} async-done(((f32[64,8,512]{2,1,0:T(8,128)}), f32[64,8,512]{2,1,0:T(8,128)S(1)}, u32[]{:S(2)}, u32[]{:S(2)}) %all-to-all-start.2) | async-done | bytes 1048608 | tf_op jit(solution)/shard_map/all_to_all | solution.py:18
  77.2 4.5 %gather_fusion = f32[512]{0:T(512)S(1)} fusion(f32[512,512]{1,0:T(8,128)S(1)} %bitcast.144, s32[512]{0:T(512)S(1)} %bitcast.143), kind=kCustom, calls=%fused_computation | custom fusion | bytes 8192 | tf_op jit(solution)/shard_map/jit(diagonal)/cond/branch_0_fun/gather | solution.py:96
  81.8 1.9 select_subtract_fusion.1
  83.6 3.6 %fusion.6 = f32[512,512]{1,0:T(8,128)S(1)} fusion(f32[512,512]{0,1:T(8,128)S(1)} %select_subtract_fusion.1, f32[512]{0:T(512)S(1)} %gather_fusion), kind=kOutput, calls=%fused_computation.24 | convolution fusion | flops 1611399168 | bytes 2099200 | tf_op jit(solution)/shard_map/dot_general | solution.py:98
  87.2 3.5 %select_subtract_fusion = f32[512,512]{0,1:T(8,128)S(1)} fusion(f32[512,512]{1,0:T(8,128)S(1)} %fusion.6, f32[64,8,512]{2,1,0:T(8,128)S(1)} %all-to-all-done.2), kind=kOutput, calls=%fused_computation.11 | convolution fusion | flops 1611399168 | bytes 3145728 | tf_op jit(solution)/shard_map/dot_general | solution.py:98
  90.7 1.9 fusion.43
  92.6 0.5 convolution_convert_fusion.5
  93.1 0.4 fusion.3
  93.5 0.8 maximum_maximum_fusion
  94.3 0.2 all-gather.5.cloned.1.call-start
  94.6 45.0 %all-gather.3.cloned.1.call-done = bf16[8,2,192,512]{3,2,1,0:T(8,128)(2,1)} async-done(((bf16[1,2,192,512]{3,2,1,0:T(8,128)(2,1)}), bf16[8,2,192,512]{3,2,1,0:T(8,128)(2,1)}) %all-gather.3.cloned.1.call-update) | async-done | bytes 3145744 | tf_op jit(solution)/shard_map/all_gather | solution.py:44
  139.6 2.1 slice_bitcast_fusion.1
  141.7 0.9 copy.35
  142.6 0.9 copy.37
  143.5 0.6 convolution_convert_fusion.3
  144.1 0.6 convolution_convert_fusion.2
  144.7 0.1 copy_bitcast_fusion
  144.8 0.9 pad_maximum_fusion
  145.8 44.9 %all-gather.5.cloned.1.call-done = bf16[4,8,192,512]{3,2,0,1:T(8,128)(2,1)} async-done(((bf16[4,1,192,512]{3,2,0,1:T(8,128)(2,1)}), bf16[4,8,192,512]{3,2,0,1:T(8,128)(2,1)}) %all-gather.5.cloned.1.call-update) | async-done | bytes 6291472 | tf_op jit(solution)/shard_map/all_gather | solution.py:44
  190.8 3.4 %fusion.40 = (bf16[2,8,192,512]{3,2,0,1:T(8,128)(2,1)S(1)}, bf16[2,8,192,512]{3,2,0,1:T(8,128)(2,1)S(1)}) fusion(bf16[4,8,192,512]{3,2,0,1:T(8,128)(2,1)} %all-gather.5.cloned.1.call-done), kind=kLoop, calls=%fused_computation.73 | loop fusion | bytes 12582912 | tf_op jit(solution)/shard_map/split | solution.py:45
  194.1 1.8 copy.29
  195.9 1.9 fusion.1
  197.8 2.4 reshape.205
  200.2 1.8 copy.28
  202.0 1.0 fusion
  203.0 1.4 reshape.203
  204.5 2.0 convolution_convert_fusion.4
  206.4 0.1 constant_dynamic-slice_fusion
  206.5 3.1 %collective-permute-start = (bf16[2,1,512,512]{3,2,1,0:T(8,128)(2,1)S(1)}, bf16[2,1,512,512]{3,2,1,0:T(8,128)(2,1)}, u32[]{:S(2)}, u32[]{:S(2)}) collective-permute-start(bf16[2,1,512,512]{3,2,1,0:T(8,128)(2,1)S(1)} %constant_dynamic-slice_fusion), channel_id=1, source_target_pairs={{0,64},{64,0},{128,192},{192,128},{256,320},{320,256},{384,448},{4... | collective-permute-start | bytes 3145736 | tf_op jit(solution)/shard_map/ppermute | solution.py:49
  209.6 23.3 %collective-permute-done = bf16[2,1,512,512]{3,2,1,0:T(8,128)(2,1)} collective-permute-done((bf16[2,1,512,512]{3,2,1,0:T(8,128)(2,1)S(1)}, bf16[2,1,512,512]{3,2,1,0:T(8,128)(2,1)}, u32[]{:S(2)}, u32[]{:S(2)}) %collective-permute-start) | collective-permute-done | bytes 1048608 | tf_op jit(solution)/shard_map/ppermute | solution.py:49
  233.0 2.5 %fusion.5 = bf16[1,2,1,512,512]{4,3,2,1,0:T(8,128)(2,1)} fusion(bf16[2,1,512,512]{3,2,1,0:T(8,128)(2,1)} %collective-permute-done, bf16[2,2,512,512]{3,2,1,0:T(8,128)(2,1)S(1)} %convolution_convert_fusion.4, s32[]{:T(128)S(6)} %select_n.76), kind=kLoop, calls=%fused_computation.21 | loop fusion | flops 2097152 | bytes 3145732 | tf_op jit(solution)/shard_map/broadcast_in_dim | solution.py:138
  (17 shorter events, 0.1 us)
Async XLA Ops:
  8.1 16.6 %all-to-all-start.1 = ((bf16[8,64,192]{2,1,0:T(8,128)(2,1)}), bf16[8,64,192]{2,1,0:T(8,128)(2,1)S(1)}, u32[]{:S(2)}, u32[]{:S(2)}) async-start(bf16[8,64,192]{2,1,0:T(8,128)(2,1)} %stack.5), calls=%async_computation.1 | async-start | bytes 524288 | tf_op jit(solution)/shard_map/all_to_all | solution.py:30
  18.2 32.7 %copy-start.1 = (bf16[1,1,1,96,512]{4,3,2,1,0:T(8,128)(2,1)S(1)}, bf16[1,1,1,96,512]{4,3,2,1,0:T(8,128)(2,1)}, u32[]{:S(2)}) copy-start(bf16[1,1,1,96,512]{4,3,2,1,0:T(8,128)(2,1)} %param.18) | copy-start | bytes 294916
  18.2 32.8 %copy-start.2 = (bf16[1,1,1,96,512]{4,3,2,1,0:T(8,128)(2,1)S(1)}, bf16[1,1,1,96,512]{4,3,2,1,0:T(8,128)(2,1)}, u32[]{:S(2)}) copy-start(bf16[1,1,1,96,512]{4,3,2,1,0:T(8,128)(2,1)} %param.19) | copy-start | bytes 294916
  42.2 35.1 %all-to-all-start.2 = ((f32[64,8,512]{2,1,0:T(8,128)}), f32[64,8,512]{2,1,0:T(8,128)S(1)}, u32[]{:S(2)}, u32[]{:S(2)}) async-start(f32[64,8,512]{2,1,0:T(8,128)} %broadcast_in_dim.49), calls=%async_computation.2 | async-start | bytes 2097152 | tf_op jit(solution)/shard_map/all_to_all | solution.py:18
  48.9 90.7 %all-gather.3.cloned.1.call-start = ((), (), s32[]{:S(2)}) async-start(), calls=%async_computation.3 | async-start | bytes 3538944 | tf_op jit(solution)/shard_map/all_gather | solution.py:44
  94.3 96.4 %all-gather.5.cloned.1.call-start = ((), (), s32[]{:S(2)}) async-start(), calls=%async_computation.4 | async-start | bytes 7077888 | tf_op jit(solution)/shard_map/all_gather | solution.py:44
  142.6 0.9 copy-start.3
  202.0 2.5 %copy-start = (bf16[2,2,192,512]{3,2,1,0:T(8,128)(2,1)S(1)}, bf16[2,2,192,512]{3,2,1,0:T(8,128)(2,1)}, u32[]{:S(2)}) copy-start(bf16[2,2,192,512]{3,2,1,0:T(8,128)(2,1)} %reshape.205) | copy-start | bytes 2359300
  206.5 26.5 %collective-permute-start = (bf16[2,1,512,512]{3,2,1,0:T(8,128)(2,1)S(1)}, bf16[2,1,512,512]{3,2,1,0:T(8,128)(2,1)}, u32[]{:S(2)}, u32[]{:S(2)}) collective-permute-start(bf16[2,1,512,512]{3,2,1,0:T(8,128)(2,1)S(1)} %constant_dynamic-slice_fusion), channel_id=1, source_target_pairs={{0,64},{64,0},{128,192},{192,128},{256,320},{320,256},{384,448},{4... | collective-permute-start | bytes 3145736 | tf_op jit(solution)/shard_map/ppermute | solution.py:49
Sparse Core Ops, SparseCore 0:
  94.4 45.1 all-gather.2
  145.9 44.7 all-gather.4
